TPU v7x, 32 devices: a whole 2x2x4 slice. The times are simulated.
32 devices in a mesh: samp: 4 (over x, core), feat: 8 (over z, y).
Axes of the slice: x: 2, y: 2, z: 4, core: 2. Of those that a mesh axis runs over, the one named last changes fastest.
Arguments:
- design: float32 [4096, 65536], P('samp', 'feat'), may hold values from -0.09375 to 0.09375
- coefficients: float32 [192, 65536], P(None, 'feat'), may hold values from -3 to 3
- response: float32 [192, 4096], P(None, 'samp'), may hold values from -6 to 6
- active_set: int32 [192, 65536], P(None, 'feat'), may hold values 0 or 1
- lambda_path: float32 [192, 16], P('samp'), may hold values from 0.5 to 4
- lambda_index: int32 [192], P('samp'), may hold values from 1 to 15
Outputs:
- margins: float32 [192, 65536], P('samp', 'feat')
- peak_gradient: float32 [192], P('samp')
- violation: float32 [192], P('samp')
- screen_mass: float32 [192], P('samp')
Inputs may be any that keep to these rules, and one draw needn't show every extreme that they name: `active_set`: 1 marks a feature in the response's active set, 0 one outside it. `lambda_index`: the current point on the response's path; the previous point is the one just below it.
All inputs are finite; a program needn't handle non-finite values. No bound on the sum of `active_set` on one device may be relied on, other than what follows from the above.
Results may differ from a plain program's by a relative error of at most 0.000073.
Values sent between devices are 32-bit elements; how exact they have to be, the bound alone decides.
A program may use at most 128 MiB of HBM per device.

v0:
```python
import jax
import jax.numpy as jnp
from jax import lax
from jax.sharding import PartitionSpec as P

NF = 65536


def body(design, coefficients, response, active_set, lambda_path, lambda_index):
    masked = coefficients * active_set.astype(jnp.float32)
    partial_value = lax.dot_general(
        masked,
        design,
        (((1,), (1,)), ((), ())),
        precision=lax.Precision.HIGHEST,
        preferred_element_type=jnp.float32,
    )
    fitted = lax.psum(partial_value, "feat")
    residual = response - fitted
    share_rows = lambda_path.shape[0]
    own_first = lax.axis_index("samp") * share_rows
    gradient = lax.psum_scatter(
        jnp.dot(
            residual, design, precision=lax.Precision.HIGHEST, preferred_element_type=jnp.float32
        ),
        "samp",
        scatter_dimension=0,
        tiled=True,
    )
    own_active = lax.dynamic_slice_in_dim(active_set, own_first, share_rows, 0)
    positions = jnp.arange(lambda_path.shape[1], dtype=jnp.int32)
    picker_now = (positions[None, :] == lambda_index[:, None]).astype(jnp.float32)
    picker_before = (positions[None, :] == lambda_index[:, None] - 1).astype(jnp.float32)
    lambda_new = jnp.sum(lambda_path * picker_now, axis=1)
    lambda_old = jnp.sum(lambda_path * picker_before, axis=1)
    threshold = 2.0 * lambda_new - lambda_old
    magnitude = jnp.abs(gradient)
    margins = magnitude - threshold[:, None]
    local_peak = jnp.max(magnitude, axis=1)
    inactive = 1.0 - own_active.astype(jnp.float32)
    local_violation = (
        jnp.sum(inactive * jnp.maximum(magnitude - lambda_new[:, None], 0.0), axis=1) / NF
    )
    local_mass = jnp.sum(jnp.maximum(margins, 0.0), axis=1) / NF
    peak_gradient = lax.pmax(local_peak, "feat")
    violation, screen_mass = lax.psum((local_violation, local_mass), "feat")
    return (margins, peak_gradient, violation, screen_mass)


def solution(mesh):
    return jax.shard_map(
        body,
        mesh=mesh,
        in_specs=(
            P("samp", "feat"),
            P(None, "feat"),
            P(None, "samp"),
            P(None, "feat"),
            P("samp", None),
            P("samp"),
        ),
        out_specs=(P("samp", "feat"), P("samp"), P("samp"), P("samp")),
        check_vma=False,
    )
```

profile of v0, /device:TPU:0, one launch (start us, length us, event | category | flops | bytes accessed | tf_op | source)
XLA Modules:
  0.0 260.9 jit_solution(6805318242318605775)
XLA Ops:
  7.2 0.0 copy-start
  7.2 0.0 all-reduce.3.cloned.1.call-start
  7.2 39.6 %fusion = f32[192,1024]{1,0:T(8,128)} fusion(f32[1024,8192]{1,0:T(8,128)} %param.6, f32[192,8192]{1,0:T(8,128)} %param.7, s32[192,8192]{1,0:T(8,128)} %param.9), kind=kOutput, calls=%fused_computation | convolution fusion | flops 19330498560 | bytes 46923776 | tf_op jit(solution)/shard_map/dot_general | solution.py:11
  46.8 0.0 all-reduce.3.cloned.1.call-update
  46.8 0.2 reduce-scatter.2.cloned.1.call-start
  47.0 77.7 %all-reduce.3.cloned.1.call-done = f32[192,1024]{1,0:T(8,128)} async-done(((f32[192,1024]{1,0:T(8,128)}), f32[192,1024]{1,0:T(8,128)}) %all-reduce.3.cloned.1.call-update) | async-done | bytes 786448 | tf_op jit(solution)/shard_map/psum | solution.py:18
  124.8 0.0 copy-done
  124.8 27.9 %fusion.3 = f32[192,8192]{1,0:T(8,128)} fusion(f32[1024,8192]{1,0:T(8,128)} %param.6, f32[192,1024]{1,0:T(8,128)S(1)} %copy-done, f32[192,1024]{1,0:T(8,128)} %all-reduce.3.cloned.1.call-done), kind=kOutput, calls=%fused_computation.7 | convolution fusion | flops 19327549440 | bytes 41418752 | tf_op jit(solution)/shard_map/dot_general | solution.py:23
  152.7 0.0 copy-start.2
  152.7 0.0 copy-start.1
  152.7 0.0 reduce-scatter.2.cloned.1.call-update
  152.7 0.6 copy-done.2
  153.3 0.1 copy-done.1
  153.4 57.4 %reduce-scatter.2.cloned.1.call-done = f32[48,8192]{1,0:T(8,128)} async-done(((f32[192,8192]{1,0:T(8,128)}), f32[48,8192]{1,0:T(8,128)}) %reduce-scatter.2.cloned.1.call-update) | async-done | bytes 1572880 | tf_op jit(solution)/shard_map/reduce_scatter | solution.py:22
  210.9 3.7 %multiply_reduce_fusion = (f32[48]{0:T(128)S(1)}, f32[48]{0:T(128)S(1)}, f32[48]{0:T(128)S(1)}, f32[48,8192]{1,0:T(8,128)}) fusion(s32[192,8192]{1,0:T(8,128)} %param.9, s32[]{:T(128)S(6)} %select_n.3, f32[48,8192]{1,0:T(8,128)} %reduce-scatter.2.cloned.1.call-done, f32[48]{0:T(128)S(1)} %get-tuple-element.6, f32[48]{0:T(128)S(1)} %multiply_subtract_fusion), kind=kLoop, calls=%fused_computation.4 | loop fusion | flops 4325232 | bytes 4719556 | tf_op jit(solution)/shard_map/reduce_sum | solution.py:42
  214.6 21.9 %pmax.7 = f32[48]{0:T(128)} all-reduce(f32[48]{0:T(128)S(1)} %get-tuple-element.5), channel_id=1, replica_groups=mesh['samp'=4,'feat'=8] {'feat'}, use_global_device_ids=true, to_apply=%region_5.0 | all-reduce | flops 48 | bytes 384 | tf_op jit(solution)/shard_map/pmax | solution.py:45
  236.5 17.6 %all-reduce = (f32[48]{0:T(128)}, f32[48]{0:T(128)}) all-reduce(f32[48]{0:T(128)S(1)} %get-tuple-element.15, f32[48]{0:T(128)S(1)} %get-tuple-element.14), channel_id=1, replica_groups=mesh['samp'=4,'feat'=8] {'feat'}, use_global_device_ids=true, to_apply=%region_7.0 | all-reduce | flops 96 | bytes 768 | tf_op jit(solution)/shard_map/psum | solution.py:46
  (4 shorter events, 0.0 us)
Async XLA Ops:
  7.2 117.6 %copy-start = (f32[192,1024]{1,0:T(8,128)S(1)}, f32[192,1024]{1,0:T(8,128)}, u32[]{:S(2)}) copy-start(f32[192,1024]{1,0:T(8,128)} %param.8) | copy-start | bytes 2359300
  7.2 117.6 %all-reduce.3.cloned.1.call-start = ((), (), s32[]{:S(2)}) async-start(), calls=%async_computation.1 | async-start | bytes 1572864 | tf_op jit(solution)/shard_map/psum | solution.py:18
  46.8 164.1 %reduce-scatter.2.cloned.1.call-start = ((), (), s32[]{:S(2)}) async-start(), calls=%async_computation.2 | async-start | bytes 7864320 | tf_op jit(solution)/shard_map/reduce_scatter | solution.py:22
  152.7 0.7 copy-start.2
  152.7 0.7 copy-start.1
Sparse Core Ops, SparseCore 0:
  46.9 77.7 all-reduce.2
  152.8 57.9 reduce-scatter.1
where the time goes:
time: 261 us
  waiting for transfers between devices  135 us (52%)
  matrix products  67.5 us (26%)
  blocking collectives  39.5 us (15%)
  between operations  14.1 us (5%)
  other arithmetic  3.78 us (1%)
    psum x1, waiting for transfers between devices, body(): fitted = lax.psum(partial_value, 'feat')  77.7 us
    reduce_scatter x1, waiting for transfers between devices, body(): lax.psum_scatter(jnp.dot(residual, design, precision=lax.Precision.HIGHES...  57.4 us
    dot_general x1, matrix products, body(): lax.dot_general(masked, design, (((1,), (1,)), ((), ())), precision=lax.P...  39.6 us
    dot_general x1, matrix products, body(): jnp.dot(residual, design, precision=lax.Precision.HIGHEST, preferred_elem...  27.9 us
    pmax x1, blocking collectives, body(): peak_gradient = lax.pmax(local_peak, 'feat')  21.9 us
    psum x1, blocking collectives, body(): violation, screen_mass = lax.psum((local_violation, local_mass), 'feat')  17.6 us
  transfers between devices with their start and end apart: 2, of which 2 were waited for; matrix products, arithmetic and copies ran while one was open for 0% of the time, Pallas kernels for 0%

commit v1 on v0

v1 whole, which is shorter than its diff:
```python
import functools

import jax
import jax.numpy as jnp
from jax import lax
from jax.experimental import pallas as pl
from jax.experimental.pallas import tpu as pltpu
from jax.sharding import PartitionSpec as P

MESH = pl.DeviceIdType.MESH
F32 = jnp.float32
BF16 = jnp.bfloat16
CHUNK = 256
TILE = 256
PIECE = 32
SLOTS = 4
CROWS = 48


def split(v):
    hi = v.astype(BF16)
    return hi, (v - hi.astype(F32)).astype(BF16)


def nt(a, b):
    return lax.dot_general(a, b, (((1,), (1,)), ((), ())), preferred_element_type=F32)


def kernel(
    cfg,
    design, coef, active, response, path, index,
    margins, stats_out,
    dh, dl, mm, stage, cst, ast, gb, crecv, xrecv, aown,
    part, yrecv, ysum, zrecv, full, resp, rr, sown, srecv,
    stage_sem, coef_sem, act_sem, resp_sem, aown_sem, out_sem,
    y_send, y_recv, z_send, z_recv, az_send, az_recv, ay_send, ay_recv,
    c_send, c_recv, x_send, x_recv, s_send, s_recv,
):
    S, F, A, B, X, R, rf, rp, rs, SL, FL = cfg
    Rp = F * rp
    C = SL // CHUNK
    T = FL // TILE
    KB = CHUNK // PIECE
    KW = FL // KB
    s = lax.axis_index("samp")
    f = lax.axis_index("feat")
    z = f // A
    y = f % A
    x = s // 2
    core = s % 2

    def padded(v):
        if rf == rp:
            return v
        fill = jnp.zeros((rp - rf, v.shape[1]), v.dtype)
        out = []
        for q in range(v.shape[0] // rf):
            out += [v[q * rf : (q + 1) * rf], fill]
        return jnp.concatenate(out, axis=0)

    barrier = pltpu.get_barrier_semaphore()
    peers = [(s, lax.rem(f + k, F)) for k in range(1, F)]
    peers += [(x * 2 + 1 - core, f)]
    peers += [(lax.rem(x + k, X) * 2 + core, f) for k in range(1, X)]
    for peer in peers:
        pl.semaphore_signal(barrier, inc=1, device_id=peer, device_id_type=MESH)

    half = FL // 2

    def coef_copies(i):
        rows = pl.ds((i // 2) * CROWS, CROWS)
        cols = pl.ds((i % 2) * half, half)
        return (
            pltpu.make_async_copy(coef.at[rows, cols], cst.at[i % 2], coef_sem.at[i % 2]),
            pltpu.make_async_copy(active.at[rows, cols], ast.at[i % 2], act_sem.at[i % 2]),
        )

    def piece_copy(p, slot):
        rows = pl.ds(pl.multiple_of(p * PIECE, PIECE), PIECE)
        return pltpu.make_async_copy(design.at[rows, :], stage.at[slot], stage_sem.at[slot])

    nc = 2 * R // CROWS
    NP = SL // PIECE
    for i in range(2):
        for cp in coef_copies(i):
            cp.start()
    for p in range(SLOTS):
        piece_copy(p, p).start()
    resp_copy = pltpu.make_async_copy(response, resp, resp_sem)
    for i in range(nc):
        for cp in coef_copies(i):
            cp.wait()
        m0 = (i // 2) * CROWS // rf * rp
        mr = CROWS // rf * rp
        step = 1024 if half % 1024 == 0 else half

        def mask_cols(j, carry, i=i, m0=m0, mr=mr, step=step):
            cols = pl.ds(pl.multiple_of(j * step, step), step)
            v = cst[i % 2, :, cols] * ast[i % 2, :, cols].astype(F32)
            hi, lo = split(padded(v))
            dst = pl.ds(pl.multiple_of((i % 2) * half + j * step, step), step)
            mm[m0 : m0 + mr, dst] = hi
            mm[Rp + m0 : Rp + m0 + mr, dst] = lo
            return carry

        lax.fori_loop(0, half // step, mask_cols, 0)
        if i + 2 < nc:
            for cp in coef_copies(i + 2):
                cp.start()
    resp_copy.start()
    own_first = pl.multiple_of(s * rs, 8)
    aown_copy = pltpu.make_async_copy(active.at[pl.ds(own_first, rs), :], aown, aown_sem)

    def split_piece(p):
        slot = lax.rem(p, SLOTS)
        piece_copy(p, slot).wait()
        rows = pl.ds(pl.multiple_of(p * PIECE, PIECE), PIECE)
        hi, lo = split(stage[slot])
        dh[rows, :] = hi
        dl[rows, :] = lo

    def next_piece(p):
        @pl.when(p + SLOTS < NP)
        def _():
            piece_copy(p + SLOTS, lax.rem(p, SLOTS)).start()

    def first_pieces(p, carry):
        split_piece(p)
        next_piece(p)
        return carry

    lax.fori_loop(0, KB, first_pieces, 0)
    pl.semaphore_wait(barrier, len(peers))

    def y_copy(c, k):
        to = lax.rem(y + k, A)
        return pltpu.make_async_remote_copy(
            part.at[c, to], yrecv.at[c, k - 1], y_send.at[c, k - 1], y_recv.at[c, k - 1],
            device_id=(s, z * A + to), device_id_type=MESH)

    def z_copy(c, k):
        to = lax.rem(z + k, B)
        return pltpu.make_async_remote_copy(
            ysum.at[c, to], zrecv.at[c, k - 1], z_send.at[c, k - 1], z_recv.at[c, k - 1],
            device_id=(s, to * A + y), device_id_type=MESH)

    def az_copy(c, k):
        to = lax.rem(z + k, B)
        return pltpu.make_async_remote_copy(
            full.at[c, y, z], full.at[c, y, z], az_send.at[c, k - 1], az_recv.at[c, k - 1],
            device_id=(s, to * A + y), device_id_type=MESH)

    def ay_copy(c, k):
        to = lax.rem(y + k, A)
        return pltpu.make_async_remote_copy(
            full.at[c, y], full.at[c, y], ay_send.at[c, k - 1], ay_recv.at[c, k - 1],
            device_id=(s, z * A + to), device_id_type=MESH)

    def stage1(c):
        for k in range(1, A):
            y_copy(c, k).start()

    def stage2(c):
        total = part[c, y]
        for k in range(1, A):
            y_copy(c, k).wait_recv()
            total = total + yrecv[c, k - 1]
        ysum[c] = total
        for k in range(1, B):
            z_copy(c, k).start()

    def stage3(c):
        total = ysum[c, z]
        for k in range(1, B):
            z_copy(c, k).wait_recv()
            total = total + zrecv[c, k - 1]
        full[c, y, z] = total
        for k in range(1, B):
            az_copy(c, k).start()

    def stage4(c):
        for k in range(1, B):
            az_copy(c, k).wait_recv()
        for k in range(1, A):
            ay_copy(c, k).start()

    def stage5(c):
        for k in range(1, A):
            ay_copy(c, k).wait_recv()
        cols = slice(c * CHUNK, (c + 1) * CHUNK)
        fitted = full[c].reshape(Rp, CHUNK)
        hi, lo = split(padded(resp[:, cols]) - fitted)
        rr[0:Rp, cols] = hi
        rr[Rp : 2 * Rp, cols] = lo

    stages = (stage1, stage2, stage3, stage4, stage5)
    for c in range(C + 4):
        if c < C:
            def fit(j, acc, c=c):
                cols = pl.ds(pl.multiple_of(j * KW, KW), KW)
                rows = slice(c * CHUNK, (c + 1) * CHUNK)
                if c + 1 < C:
                    split_piece((c + 1) * KB + j)
                both = nt(mm[:, cols], dh[rows, cols])
                small = nt(mm[0:Rp, cols], dl[rows, cols])
                if c + 1 < C:
                    next_piece((c + 1) * KB + j)
                return acc + (both[0:Rp] + (both[Rp:] + small))

            acc = lax.fori_loop(0, KB, fit, jnp.zeros((Rp, CHUNK), F32))
            part[c] = acc.reshape(A, B, rp, CHUNK)
        if c == C - 1:
            aown_copy.start()
            resp_copy.wait()
        for n, g in enumerate(stages):
            if 0 <= c - n < C:
                g(c - n)

    def c_copy(t):
        return pltpu.make_async_remote_copy(
            gb.at[t, 1 - core], crecv.at[t], c_send.at[t], c_recv.at[t],
            device_id=(x * 2 + 1 - core, f), device_id_type=MESH)

    def x_copy(t, k):
        to = lax.rem(x + k, X)
        return pltpu.make_async_remote_copy(
            gb.at[t, core, to], xrecv.at[t, k - 1], x_send.at[t, k - 1], x_recv.at[t, k - 1],
            device_id=(to * 2 + core, f), device_id_type=MESH)

    def forward(t):
        c_copy(t).wait_recv()
        gb[t, core] = gb[t, core] + crecv[t]
        for k in range(1, X):
            x_copy(t, k).start()

    def grad(t, carry):
        cols = pl.ds(pl.multiple_of(t * TILE, TILE), TILE)
        both = jnp.dot(rr[...], dh[:, cols], preferred_element_type=F32)
        small = jnp.dot(rr[0:Rp, :], dl[:, cols], preferred_element_type=F32)
        g = both[0:Rp] + (both[Rp:] + small)
        if rf == rp:
            for o in range(S):
                gb[t, o % 2, o // 2] = g[o * rs : (o + 1) * rs]
        else:
            for q in range(F):
                o, r0 = q * rf // rs, q * rf % rs
                gb[t, o % 2, o // 2, r0 : r0 + rf, :] = g[q * rp : q * rp + rf]
        c_copy(t).start()

        @pl.when(t > 0)
        def _():
            forward(t - 1)

        return carry

    lax.fori_loop(0, T, grad, 0)
    forward(T - 1)
    aown_copy.wait()

    where = index[...]
    spots = lax.broadcasted_iota(jnp.int32, path.shape, 1)
    lam_new = jnp.sum(jnp.where(spots == where, path[...], 0.0), axis=1, keepdims=True)
    lam_old = jnp.sum(jnp.where(spots == where - 1, path[...], 0.0), axis=1, keepdims=True)
    threshold = 2.0 * lam_new - lam_old

    def out_copy(t):
        cols = pl.ds(pl.multiple_of(t * TILE, TILE), TILE)
        return pltpu.make_async_copy(xrecv.at[t, 0], margins.at[:, cols], out_sem.at[t])

    def finish(t, carry):
        peak, viol, mass = carry
        total = gb[t, core, x]
        for k in range(1, X):
            x_copy(t, k).wait_recv()
            total = total + xrecv[t, k - 1]
        cols = pl.ds(pl.multiple_of(t * TILE, TILE), TILE)
        mag = jnp.abs(total)
        mar = mag - threshold
        xrecv[t, 0] = mar
        out_copy(t).start()
        inactive = 1.0 - aown[:, cols].astype(F32)
        peak = jnp.maximum(peak, mag)
        viol = viol + inactive * jnp.maximum(mag - lam_new, 0.0)
        mass = mass + jnp.maximum(mar, 0.0)
        return peak, viol, mass

    zero = jnp.zeros((rs, TILE), F32)
    peak, viol, mass = lax.fori_loop(0, T, finish, (zero, zero, zero))
    lane = lax.broadcasted_iota(jnp.int32, (rs, 128), 1)
    peak = jnp.max(peak, axis=1, keepdims=True)
    viol = jnp.sum(viol, axis=1, keepdims=True)
    mass = jnp.sum(mass, axis=1, keepdims=True)
    mine = jnp.where(lane == 0, peak, jnp.where(lane == 1, viol, mass))
    sown[...] = mine

    def s_copy(k):
        return pltpu.make_async_remote_copy(
            sown, srecv.at[k - 1], s_send.at[k - 1], s_recv.at[k - 1],
            device_id=(s, lax.rem(f + k, F)), device_id_type=MESH)

    for k in range(1, F):
        s_copy(k).start()

    for c in range(C):
        for k in range(1, A):
            y_copy(c, k).wait_send()
            ay_copy(c, k).wait_send()
        for k in range(1, B):
            z_copy(c, k).wait_send()
            az_copy(c, k).wait_send()

    def drain(t, carry):
        c_copy(t).wait_send()
        for k in range(1, X):
            x_copy(t, k).wait_send()
        out_copy(t).wait()
        return carry

    lax.fori_loop(0, T, drain, 0)
    top, add = mine, mine
    for k in range(1, F):
        s_copy(k).wait_recv()
        top = jnp.maximum(top, srecv[k - 1])
        add = add + srecv[k - 1]
    stats_out[...] = jnp.where(lane == 0, top, add / (FL * F))
    for k in range(1, F):
        s_copy(k).wait_send()


def body(S, F, design, coefficients, response, active_set, lambda_path, lambda_index):
    SL, FL = design.shape
    R = coefficients.shape[0]
    rs = lambda_path.shape[0]
    A = 1
    while (2 * A) ** 2 <= F:
        A *= 2
    B = F // A
    X = S // 2
    rf = R // F
    rp = -(-rf // 8) * 8
    Rp = F * rp
    C, T = SL // CHUNK, FL // TILE
    cfg = (S, F, A, B, X, R, rf, rp, rs, SL, FL)
    hbm = pl.BlockSpec(memory_space=pl.ANY)
    vmem = pl.BlockSpec(memory_space=pltpu.VMEM)
    dma = pltpu.SemaphoreType.DMA
    margins, stats = pl.pallas_call(
        functools.partial(kernel, cfg),
        out_shape=(
            jax.ShapeDtypeStruct((rs, FL), F32),
            jax.ShapeDtypeStruct((rs, 128), F32),
        ),
        in_specs=[hbm, hbm, hbm, hbm, vmem, vmem],
        out_specs=(hbm, vmem),
        scratch_shapes=[
            pltpu.VMEM((SL, FL), BF16),
            pltpu.VMEM((SL, FL), BF16),
            pltpu.VMEM((2 * Rp, FL), BF16),
            pltpu.VMEM((SLOTS, PIECE, FL), F32),
            pltpu.VMEM((2, CROWS, FL // 2), F32),
            pltpu.VMEM((2, CROWS, FL // 2), jnp.int32),
            pltpu.VMEM((T, 2, X, rs, TILE), F32),
            pltpu.VMEM((T, X, rs, TILE), F32),
            pltpu.VMEM((T, max(X - 1, 1), rs, TILE), F32),
            pltpu.VMEM((rs, FL), jnp.int32),
            pltpu.VMEM((C, A, B, rp, CHUNK), F32),
            pltpu.VMEM((C, A - 1, B, rp, CHUNK), F32),
            pltpu.VMEM((C, B, rp, CHUNK), F32),
            pltpu.VMEM((C, B - 1, rp, CHUNK), F32),
            pltpu.VMEM((C, A, B, rp, CHUNK), F32),
            pltpu.VMEM((R, SL), F32),
            pltpu.VMEM((2 * Rp, SL), BF16),
            pltpu.VMEM((rs, 128), F32),
            pltpu.VMEM((F - 1, rs, 128), F32),
            dma((SLOTS,)), dma((2,)), dma((2,)), dma, dma, dma((T,)),
            dma((C, A - 1)), dma((C, A - 1)), dma((C, B - 1)), dma((C, B - 1)),
            dma((C, B - 1)), dma((C, B - 1)), dma((C, A - 1)), dma((C, A - 1)),
            dma((T,)), dma((T,)), dma((T, X - 1)), dma((T, X - 1)),
            dma((F - 1,)), dma((F - 1,)),
        ],
        compiler_params=pltpu.CompilerParams(
            collective_id=0, has_side_effects=True, vmem_limit_bytes=67043328
        ),
    )(
        design, coefficients, active_set, response, lambda_path,
        lambda_index.reshape(rs, 1),
    )
    return margins, stats[:, 0], stats[:, 1], stats[:, 2]


def solution(mesh):
    return jax.shard_map(
        functools.partial(body, mesh.shape["samp"], mesh.shape["feat"]),
        mesh=mesh,
        in_specs=(
            P("samp", "feat"),
            P(None, "feat"),
            P(None, "samp"),
            P(None, "feat"),
            P("samp", None),
            P("samp"),
        ),
        out_specs=(P("samp", "feat"), P("samp"), P("samp"), P("samp")),
        check_vma=False,
    )
```

time: 261 us -> 109 us (0.42)
  waiting for transfers between devices: 135 us -> 0 us
  Pallas kernels: 0 us -> 101 us
  matrix products: 67.5 us -> 0 us
  blocking collectives: 39.5 us -> 0 us
  between operations: 14.1 us -> 0.64 us
  local copies, waits for them, and re-layouts: 0.68 us -> 6.96 us
  other arithmetic: 3.78 us -> 0 us
    pallas_call x0 -> x1, Pallas kernels: none -> 101 us  [body(): pl.pallas_call(functools.partial(kernel, cfg), out_shape=(jax.ShapeDtypeS...]
    psum x1 -> x0, waiting for transfers between devices: 77.7 us -> none  [body(): fitted = lax.psum(partial_value, 'feat')]
    dot_general x2 -> x0, matrix products: 67.5 us -> none  [the longest x1 39.6 us: body(): lax.dot_general(masked, design, (((1,), (1,)), ((), ())), precision=lax.P...]
    reduce_scatter x1 -> x0, waiting for transfers between devices: 57.4 us -> none  [body(): lax.psum_scatter(jnp.dot(residual, design, precision=lax.Precision.HIGHES...]
    pmax x1 -> x0, blocking collectives: 21.9 us -> none  [body(): peak_gradient = lax.pmax(local_peak, 'feat')]
    psum x1 -> x0, blocking collectives: 17.6 us -> none  [body(): violation, screen_mass = lax.psum((local_violation, local_mass), 'feat')]
    reduce_sum x2 -> x0, other arithmetic: 3.77 us -> none  [the longest x1 3.75 us: body(): jnp.sum(inactive * jnp.maximum(magnitude - lambda_new[:, None], 0.0), axi...]
    unnamed x6 -> x2, local copies, waits for them, and re-layouts: 0.68 us -> 4.03 us
  transfers between devices with their start and end apart: 2 -> 0, of which waited for: 2 -> 0; matrix products, arithmetic and copies ran while one was open for 0% -> 0% of each run, Pallas kernels for 0% -> 0%
where the time goes in v1:
time: 109 us; the launch traced here: 108 us
  Pallas kernels  101 us (93%)
  local copies, waits for them, and re-layouts  6.96 us (6%)
    pallas_call x1, Pallas kernels, body(): pl.pallas_call(functools.partial(kernel, cfg), out_shape=(jax.ShapeDtypeS...  101 us
    unnamed x2, local copies, waits for them, and re-layouts  4.03 us

profile of v1, /device:TPU:0, one launch (start us, length us, event | category | flops | bytes accessed | tf_op | source)
XLA Modules:
  0.0 108.2 jit_solution(7594409619249100541)
XLA Ops:
  0.6 1.4 %copy.12.path = f32[48,16]{1,0:T(8,128)} copy(f32[48,16]{0,1:T(8,128)} %param.10) | data formatting | bytes 6144 | tf_op args[4]
  2.0 1.3 %copy.13.index = s32[48,1]{1,0:T(8,128)} copy(s32[48,1]{0,1:T(1,128)} %bitcast.1) | data formatting | bytes 384 | tf_op jit(solution)/shard_map/reshape | solution.py:386
  3.4 100.6 %shard_map.93 = (f32[48,8192]{1,0:T(8,128)}, f32[48,128]{1,0:T(8,128)}) custom-call(f32[1024,8192]{1,0:T(8,128)} %design.1, f32[192,8192]{1,0:T(8,128)} %coef.1, s32[192,8192]{1,0:T(8,128)} %active.1, f32[192,1024]{1,0:T(8,128)} %response.1, f32[48,16]{1,0:T(8,128)} %copy.12.path, s32[48,1]{1,0:T(8,128)} %copy.13.index), custom_call_target="tpu_custom_call" | custom-call | tf_op jit(solution)/shard_map/pallas_call | solution.py:347
  104.0 1.6 %slice_reduce_fusion = (f32[48]{0:T(128)}, f32[48]{0:T(128)}, f32[48]{0:T(128)}) fusion(f32[48,128]{1,0:T(8,128)} %get-tuple-element.7), kind=kLoop, calls=%fused_computation | loop fusion | bytes 1152 | tf_op jit(solution)/shard_map/slice | solution.py:388
  105.6 2.7 %copy.15 = f32[48,8192]{1,0:T(8,128)} copy(f32[48,8192]{1,0:T(8,128)} %get-tuple-element.15) | data formatting | bytes 3145728

commit v2 on v1

--- a/solution.py
+++ b/solution.py
@@ -11,6 +11,8 @@
 F32 = jnp.float32
 BF16 = jnp.bfloat16
 CHUNK = 256
+WIDE = 128
+STEPS = 4
 TILE = 256
 PIECE = 32
 SLOTS = 4
@@ -30,18 +32,21 @@
     cfg,
     design, coef, active, response, path, index,
     margins, stats_out,
-    dh, dl, mm, stage, cst, ast, gb, crecv, xrecv, aown,
+    parts, mm, stage, cst, ast, gb, crecv, xrecv, aown, pathv, indexv,
     part, yrecv, ysum, zrecv, full, resp, rr, sown, srecv,
-    stage_sem, coef_sem, act_sem, resp_sem, aown_sem, out_sem,
+    stage_sem, coef_sem, act_sem, resp_sem, aown_sem, path_sem, index_sem, out_sem,
     y_send, y_recv, z_send, z_recv, az_send, az_recv, ay_send, ay_recv,
     c_send, c_recv, x_send, x_recv, s_send, s_recv,
 ):
     S, F, A, B, X, R, rf, rp, rs, SL, FL = cfg
     Rp = F * rp
     C = SL // CHUNK
+    V = CHUNK // WIDE
     T = FL // TILE
     KB = CHUNK // PIECE
-    KW = FL // KB
+    KW = FL // STEPS
+    PS = KB // STEPS
+    dh, dl = parts[:C], parts[C:]
     s = lax.axis_index("samp")
     f = lax.axis_index("feat")
     z = f // A
@@ -87,6 +92,8 @@
     for p in range(SLOTS):
         piece_copy(p, p).start()
     resp_copy = pltpu.make_async_copy(response, resp, resp_sem)
+    path_copy = pltpu.make_async_copy(path, pathv, path_sem)
+    index_copy = pltpu.make_async_copy(index, indexv, index_sem)
     for i in range(nc):
         for cp in coef_copies(i):
             cp.wait()
@@ -108,16 +115,19 @@
             for cp in coef_copies(i + 2):
                 cp.start()
     resp_copy.start()
+    path_copy.start()
+    index_copy.start()
     own_first = pl.multiple_of(s * rs, 8)
     aown_copy = pltpu.make_async_copy(active.at[pl.ds(own_first, rs), :], aown, aown_sem)
 
-    def split_piece(p):
+    def split_piece(c, j):
+        p = c * KB + j
         slot = lax.rem(p, SLOTS)
         piece_copy(p, slot).wait()
-        rows = pl.ds(pl.multiple_of(p * PIECE, PIECE), PIECE)
+        rows = pl.ds(pl.multiple_of(j * PIECE, PIECE), PIECE)
         hi, lo = split(stage[slot])
-        dh[rows, :] = hi
-        dl[rows, :] = lo
+        dh[c][rows, :] = hi
+        dl[c][rows, :] = lo
 
     def next_piece(p):
         @pl.when(p + SLOTS < NP)
@@ -125,7 +135,7 @@
             piece_copy(p + SLOTS, lax.rem(p, SLOTS)).start()
 
     def first_pieces(p, carry):
-        split_piece(p)
+        split_piece(0, p)
         next_piece(p)
         return carry
 
@@ -187,8 +197,8 @@
     def stage5(c):
         for k in range(1, A):
             ay_copy(c, k).wait_recv()
-        cols = slice(c * CHUNK, (c + 1) * CHUNK)
-        fitted = full[c].reshape(Rp, CHUNK)
+        cols = slice(c * WIDE, (c + 1) * WIDE)
+        fitted = full[c].reshape(Rp, WIDE)
         hi, lo = split(padded(resp[:, cols]) - fitted)
         rr[0:Rp, cols] = hi
         rr[Rp : 2 * Rp, cols] = lo
@@ -198,23 +208,26 @@
         if c < C:
             def fit(j, acc, c=c):
                 cols = pl.ds(pl.multiple_of(j * KW, KW), KW)
-                rows = slice(c * CHUNK, (c + 1) * CHUNK)
                 if c + 1 < C:
-                    split_piece((c + 1) * KB + j)
-                both = nt(mm[:, cols], dh[rows, cols])
-                small = nt(mm[0:Rp, cols], dl[rows, cols])
+                    for i in range(PS):
+                        split_piece(c + 1, j * PS + i)
+                both = nt(mm[:, cols], dh[c][:, cols])
+                small = nt(mm[0:Rp, cols], dl[c][:, cols])
                 if c + 1 < C:
-                    next_piece((c + 1) * KB + j)
+                    for i in range(PS):
+                        next_piece((c + 1) * KB + j * PS + i)
                 return acc + (both[0:Rp] + (both[Rp:] + small))
 
-            acc = lax.fori_loop(0, KB, fit, jnp.zeros((Rp, CHUNK), F32))
-            part[c] = acc.reshape(A, B, rp, CHUNK)
+            acc = lax.fori_loop(0, STEPS, fit, jnp.zeros((Rp, CHUNK), F32))
+            for v in range(V):
+                part[c * V + v] = acc[:, v * WIDE : (v + 1) * WIDE].reshape(A, B, rp, WIDE)
         if c == C - 1:
             aown_copy.start()
             resp_copy.wait()
         for n, g in enumerate(stages):
             if 0 <= c - n < C:
-                g(c - n)
+                for v in range(V):
+                    g((c - n) * V + v)
 
     def c_copy(t):
         return pltpu.make_async_remote_copy(
@@ -235,8 +248,12 @@
 
     def grad(t, carry):
         cols = pl.ds(pl.multiple_of(t * TILE, TILE), TILE)
-        both = jnp.dot(rr[...], dh[:, cols], preferred_element_type=F32)
-        small = jnp.dot(rr[0:Rp, :], dl[:, cols], preferred_element_type=F32)
+        both = jnp.zeros((2 * Rp, TILE), F32)
+        small = jnp.zeros((Rp, TILE), F32)
+        for c in range(C):
+            ks = slice(c * CHUNK, (c + 1) * CHUNK)
+            both += jnp.dot(rr[:, ks], dh[c][:, cols], preferred_element_type=F32)
+            small += jnp.dot(rr[0:Rp, ks], dl[c][:, cols], preferred_element_type=F32)
         g = both[0:Rp] + (both[Rp:] + small)
         if rf == rp:
             for o in range(S):
@@ -257,10 +274,14 @@
     forward(T - 1)
     aown_copy.wait()
 
-    where = index[...]
+    path_copy.wait()
+    index_copy.wait()
+    down = lax.broadcasted_iota(jnp.int32, (rs, rs), 0)
+    across = lax.broadcasted_iota(jnp.int32, (rs, rs), 1)
+    where = jnp.sum(jnp.where(down == across, indexv[...], 0), axis=1, keepdims=True)
     spots = lax.broadcasted_iota(jnp.int32, path.shape, 1)
-    lam_new = jnp.sum(jnp.where(spots == where, path[...], 0.0), axis=1, keepdims=True)
-    lam_old = jnp.sum(jnp.where(spots == where - 1, path[...], 0.0), axis=1, keepdims=True)
+    lam_new = jnp.sum(jnp.where(spots == where, pathv[...], 0.0), axis=1, keepdims=True)
+    lam_old = jnp.sum(jnp.where(spots == where - 1, pathv[...], 0.0), axis=1, keepdims=True)
     threshold = 2.0 * lam_new - lam_old
 
     def out_copy(t):
@@ -301,7 +322,7 @@
     for k in range(1, F):
         s_copy(k).start()
 
-    for c in range(C):
+    for c in range(C * V):
         for k in range(1, A):
             y_copy(c, k).wait_send()
             ay_copy(c, k).wait_send()
@@ -339,7 +360,7 @@
     rf = R // F
     rp = -(-rf // 8) * 8
     Rp = F * rp
-    C, T = SL // CHUNK, FL // TILE
+    C, T, W = SL // CHUNK, FL // TILE, SL // WIDE
     cfg = (S, F, A, B, X, R, rf, rp, rs, SL, FL)
     hbm = pl.BlockSpec(memory_space=pl.ANY)
     vmem = pl.BlockSpec(memory_space=pltpu.VMEM)
@@ -350,11 +371,10 @@
             jax.ShapeDtypeStruct((rs, FL), F32),
             jax.ShapeDtypeStruct((rs, 128), F32),
         ),
-        in_specs=[hbm, hbm, hbm, hbm, vmem, vmem],
+        in_specs=[hbm] * 6,
         out_specs=(hbm, vmem),
         scratch_shapes=[
-            pltpu.VMEM((SL, FL), BF16),
-            pltpu.VMEM((SL, FL), BF16),
+            [pltpu.VMEM((CHUNK, FL), BF16)] * (2 * C),
             pltpu.VMEM((2 * Rp, FL), BF16),
             pltpu.VMEM((SLOTS, PIECE, FL), F32),
             pltpu.VMEM((2, CROWS, FL // 2), F32),
@@ -363,18 +383,20 @@
             pltpu.VMEM((T, X, rs, TILE), F32),
             pltpu.VMEM((T, max(X - 1, 1), rs, TILE), F32),
             pltpu.VMEM((rs, FL), jnp.int32),
-            pltpu.VMEM((C, A, B, rp, CHUNK), F32),
-            pltpu.VMEM((C, A - 1, B, rp, CHUNK), F32),
-            pltpu.VMEM((C, B, rp, CHUNK), F32),
-            pltpu.VMEM((C, B - 1, rp, CHUNK), F32),
-            pltpu.VMEM((C, A, B, rp, CHUNK), F32),
+            pltpu.VMEM(lambda_path.shape, F32),
+            pltpu.VMEM((1, rs), jnp.int32),
+            pltpu.VMEM((W, A, B, rp, WIDE), F32),
+            pltpu.VMEM((W, A - 1, B, rp, WIDE), F32),
+            pltpu.VMEM((W, B, rp, WIDE), F32),
+            pltpu.VMEM((W, B - 1, rp, WIDE), F32),
+            pltpu.VMEM((W, A, B, rp, WIDE), F32),
             pltpu.VMEM((R, SL), F32),
             pltpu.VMEM((2 * Rp, SL), BF16),
             pltpu.VMEM((rs, 128), F32),
             pltpu.VMEM((F - 1, rs, 128), F32),
-            dma((SLOTS,)), dma((2,)), dma((2,)), dma, dma, dma((T,)),
-            dma((C, A - 1)), dma((C, A - 1)), dma((C, B - 1)), dma((C, B - 1)),
-            dma((C, B - 1)), dma((C, B - 1)), dma((C, A - 1)), dma((C, A - 1)),
+            dma((SLOTS,)), dma((2,)), dma((2,)), dma, dma, dma, dma, dma((T,)),
+            dma((W, A - 1)), dma((W, A - 1)), dma((W, B - 1)), dma((W, B - 1)),
+            dma((W, B - 1)), dma((W, B - 1)), dma((W, A - 1)), dma((W, A - 1)),
             dma((T,)), dma((T,)), dma((T, X - 1)), dma((T, X - 1)),
             dma((F - 1,)), dma((F - 1,)),
         ],
@@ -383,7 +405,7 @@
         ),
     )(
         design, coefficients, active_set, response, lambda_path,
-        lambda_index.reshape(rs, 1),
+        lambda_index.reshape(1, rs),
     )
     return margins, stats[:, 0], stats[:, 1], stats[:, 2]
 

time: 109 us -> 103 us (0.945)
  Pallas kernels: 101 us -> 96.5 us
  local copies, waits for them, and re-layouts: 6.96 us -> 5.62 us
    pallas_call x1, Pallas kernels: 101 us -> 96.5 us  [body(): pl.pallas_call(functools.partial(kernel, cfg), out_shape=(jax.ShapeDtypeS...]
    reshape x1 -> x0, local copies, waits for them, and re-layouts: 1.34 us -> none  [body(): lambda_index.reshape(rs, 1)]
where the time goes in v2:
time: 103 us
  Pallas kernels  96.5 us (94%)
  local copies, waits for them, and re-layouts  5.62 us (5%)
    pallas_call x1, Pallas kernels, body(): pl.pallas_call(functools.partial(kernel, cfg), out_shape=(jax.ShapeDtypeS...  96.5 us
    unnamed x2, local copies, waits for them, and re-layouts  4.03 us

profile of v2, /device:TPU:0, one launch (start us, length us, event | category | flops | bytes accessed | tf_op | source)
XLA Modules:
  0.0 102.8 jit_solution(1228244280280835671)
XLA Ops:
  0.6 1.4 %copy.11.path = f32[48,16]{1,0:T(8,128)} copy(f32[48,16]{0,1:T(8,128)} %param.10) | data formatting | bytes 6144 | tf_op args[4]
  2.0 96.5 %shard_map.93 = (f32[48,8192]{1,0:T(8,128)}, f32[48,128]{1,0:T(8,128)}) custom-call(f32[1024,8192]{1,0:T(8,128)} %design.1, f32[192,8192]{1,0:T(8,128)} %coef.1, s32[192,8192]{1,0:T(8,128)} %active.1, f32[192,1024]{1,0:T(8,128)} %response.1, f32[48,16]{1,0:T(8,128)} %copy.11.path, s32[1,48]{1,0:T(1,128)} %bitcast.1), custom_call_target="tpu_custom_call" | custom-call | tf_op jit(solution)/shard_map/pallas_call | solution.py:368
  98.5 1.6 %slice_reduce_fusion = (f32[48]{0:T(128)}, f32[48]{0:T(128)}, f32[48]{0:T(128)}) fusion(f32[48,128]{1,0:T(8,128)} %get-tuple-element.7), kind=kLoop, calls=%fused_computation | loop fusion | bytes 1152 | tf_op jit(solution)/shard_map/slice | solution.py:410
  100.1 2.7 %copy.13 = f32[48,8192]{1,0:T(8,128)} copy(f32[48,8192]{1,0:T(8,128)} %get-tuple-element.15) | data formatting | bytes 3145728

commit v3 on v2

--- a/solution.py
+++ b/solution.py
@@ -120,10 +120,12 @@
     own_first = pl.multiple_of(s * rs, 8)
     aown_copy = pltpu.make_async_copy(active.at[pl.ds(own_first, rs), :], aown, aown_sem)
 
+    def wait_piece(c, j):
+        p = c * KB + j
+        piece_copy(p, lax.rem(p, SLOTS)).wait()
+
     def split_piece(c, j):
-        p = c * KB + j
-        slot = lax.rem(p, SLOTS)
-        piece_copy(p, slot).wait()
+        slot = lax.rem(c * KB + j, SLOTS)
         rows = pl.ds(pl.multiple_of(j * PIECE, PIECE), PIECE)
         hi, lo = split(stage[slot])
         dh[c][rows, :] = hi
@@ -135,6 +137,7 @@
             piece_copy(p + SLOTS, lax.rem(p, SLOTS)).start()
 
     def first_pieces(p, carry):
+        wait_piece(0, p)
         split_piece(0, p)
         next_piece(p)
         return carry
@@ -210,10 +213,12 @@
                 cols = pl.ds(pl.multiple_of(j * KW, KW), KW)
                 if c + 1 < C:
                     for i in range(PS):
-                        split_piece(c + 1, j * PS + i)
+                        wait_piece(c + 1, j * PS + i)
                 both = nt(mm[:, cols], dh[c][:, cols])
                 small = nt(mm[0:Rp, cols], dl[c][:, cols])
                 if c + 1 < C:
+                    for i in range(PS):
+                        split_piece(c + 1, j * PS + i)
                     for i in range(PS):
                         next_piece((c + 1) * KB + j * PS + i)
                 return acc + (both[0:Rp] + (both[Rp:] + small))

time: 103 us -> 105 us (1.019)
  Pallas kernels: 96.5 us -> 97.9 us
    pallas_call x1, Pallas kernels: 96.5 us -> 97.9 us  [body(): pl.pallas_call(functools.partial(kernel, cfg), out_shape=(jax.ShapeDtypeS...]
where the time goes in v3:
time: 105 us; the launch traced here: 104 us
  Pallas kernels  97.9 us (93%)
  local copies, waits for them, and re-layouts  5.62 us (5%)
    pallas_call x1, Pallas kernels, body(): pl.pallas_call(functools.partial(kernel, cfg), out_shape=(jax.ShapeDtypeS...  97.9 us
    unnamed x2, local copies, waits for them, and re-layouts  4.03 us

profile of v3, /device:TPU:0, one launch (start us, length us, event | category | flops | bytes accessed | tf_op | source)
XLA Modules:
  0.0 104.2 jit_solution(6139230306715745552)
XLA Ops:
  0.6 1.4 %copy.11.path = f32[48,16]{1,0:T(8,128)} copy(f32[48,16]{0,1:T(8,128)} %param.10) | data formatting | bytes 6144 | tf_op args[4]
  2.0 97.9 %shard_map.93 = (f32[48,8192]{1,0:T(8,128)}, f32[48,128]{1,0:T(8,128)}) custom-call(f32[1024,8192]{1,0:T(8,128)} %design.1, f32[192,8192]{1,0:T(8,128)} %coef.1, s32[192,8192]{1,0:T(8,128)} %active.1, f32[192,1024]{1,0:T(8,128)} %response.1, f32[48,16]{1,0:T(8,128)} %copy.11.path, s32[1,48]{1,0:T(1,128)} %bitcast.1), custom_call_target="tpu_custom_call" | custom-call | tf_op jit(solution)/shard_map/pallas_call | solution.py:373
  100.0 1.6 %slice_reduce_fusion = (f32[48]{0:T(128)}, f32[48]{0:T(128)}, f32[48]{0:T(128)}) fusion(f32[48,128]{1,0:T(8,128)} %get-tuple-element.7), kind=kLoop, calls=%fused_computation | loop fusion | bytes 1152 | tf_op jit(solution)/shard_map/slice | solution.py:415
  101.6 2.7 %copy.13 = f32[48,8192]{1,0:T(8,128)} copy(f32[48,8192]{1,0:T(8,128)} %get-tuple-element.15) | data formatting | bytes 3145728
